TPU v7x, 128 devices: a whole 4x4x4 slice. The times are simulated.
128 devices in a mesh: group: 4 (over x), shard: 32 (over z, y, core).
Axes of the slice: x: 4, y: 4, z: 4, core: 2. Of those that a mesh axis runs over, the one named last changes fastest.
Arguments:
- grad_pooled: bfloat16 [16384, 512, 128], P(('group', 'shard')), may hold values from -6 to 6
- bag_rows: int32 [16384, 512, 8], P(('group', 'shard')), may hold values from 0 to 511
- bag_lengths: int32 [16384, 512], P(('group', 'shard')), may hold values from 1 to 8
- table_order: int32 [512], replicated, may hold values from 0 to 511, each once
- weights: bfloat16 [512, 512, 128], P('shard'), may hold values from -6 to 6
- accum: float32 [512, 512], P('shard'), may hold values from 0.1 to 10
Outputs:
- new_weights: bfloat16 [512, 512, 128], P('shard')
- new_accum: float32 [512, 512], P('shard')
All inputs are finite; a program needn't handle non-finite values.
Results may differ from a plain program's by a relative error of at most 0.001.
Values may be sent and summed in bfloat16 or wider, within the bound.
No kernel may reach another device: no remote copies, remote signals or barrier semaphores. Data moves between devices by JAX's collectives and lax.ppermute only.
A program may use at most 128 MiB of HBM per device.

v0:
```python
import jax
import jax.numpy as jnp
from jax import lax
from jax.sharding import PartitionSpec as P

LEARN_RATE = 0.5
EPSILON = 1e-06


def expand_rows(gradient, row_ids, row_count):
    tables_first = jnp.swapaxes(gradient, 0, 1)
    picks_first = jnp.transpose(row_ids, (1, 2, 0))

    def one_table(member):
        values, chosen = member
        positions = lax.broadcasted_iota(jnp.int32, (row_count, chosen.shape[1]), 0)
        counts = jnp.zeros((row_count, chosen.shape[1]), jnp.float32)
        for column in range(chosen.shape[0]):
            counts = counts + (chosen[column][None, :] == positions).astype(jnp.float32)
        return jnp.dot(counts.astype(jnp.bfloat16), values, preferred_element_type=jnp.float32)

    return lax.map(one_table, (tables_first, picks_first))


def adagrad(weight_rows, accum_rows, row_grad):
    new_accum = accum_rows + jnp.mean(row_grad * row_grad, axis=-1)
    step_size = LEARN_RATE / (jnp.sqrt(new_accum) + EPSILON)
    new_weights = (weight_rows.astype(jnp.float32) - step_size[:, :, None] * row_grad).astype(
        jnp.bfloat16
    )
    return (new_weights, new_accum)


def body(grad_pooled, bag_rows, bag_lengths, table_order, weights, accum):
    row_count = weights.shape[1]
    bag_size = bag_rows.shape[2]
    places = lax.broadcasted_iota(jnp.int32, bag_rows.shape, 2)
    live_rows = jnp.where(places < bag_lengths[:, :, None], bag_rows, -1)
    pooled = jnp.take(grad_pooled, table_order, axis=1)
    chosen = jnp.take(live_rows, table_order, axis=1)
    groups = lax.axis_size("group")
    shards = lax.axis_size("shard")
    quarter = weights.shape[0] // groups
    samples = pooled.shape[0]
    width = pooled.shape[2]
    pooled = pooled.reshape(samples, shards, groups, quarter, width)
    pooled = jnp.transpose(pooled, (0, 2, 1, 3, 4)).reshape(
        samples, shards * groups * quarter, width
    )
    chosen = chosen.reshape(samples, shards, groups, quarter, bag_size)
    chosen = jnp.transpose(chosen, (0, 2, 1, 3, 4)).reshape(
        samples, shards * groups * quarter, bag_size
    )
    gathered = lax.all_to_all(pooled, ("group", "shard"), split_axis=1, concat_axis=0, tiled=True)
    row_ids = lax.all_to_all(chosen, ("group", "shard"), split_axis=1, concat_axis=0, tiled=True)
    row_grad = expand_rows(gathered, row_ids, row_count)
    start = lax.axis_index("group") * quarter
    weight_part = lax.dynamic_slice_in_dim(weights, start, quarter, 0)
    accum_part = lax.dynamic_slice_in_dim(accum, start, quarter, 0)
    part_weights, part_accum = adagrad(weight_part, accum_part, row_grad)
    full_weights, full_accum = (
        lax.all_gather(part_weights.astype(jnp.float32), "group", axis=0, tiled=True),
        lax.all_gather(part_accum, "group", axis=0, tiled=True),
    )
    return (full_weights.astype(jnp.bfloat16), full_accum)


def solution(mesh):
    in_specs = (
        P(("group", "shard"), None, None),
        P(("group", "shard"), None, None),
        P(("group", "shard"), None),
        P(),
        P("shard", None, None),
        P("shard", None),
    )
    out_specs = (P("shard", None, None), P("shard", None))
    return jax.shard_map(body, mesh=mesh, in_specs=in_specs, out_specs=out_specs, check_vma=False)
```

profile of v0, /device:TPU:1, one launch (start us, length us, event | category | flops | bytes accessed | tf_op | source)
XLA Modules:
  0.0 582.0 jit_solution(3212111901363523850)
XLA Ops:
  7.2 0.7 compare_select_fusion
  7.8 0.7 compare_and_fusion
  8.5 0.1 broadcast_in_dim.38
  8.7 3.1 copy.21
  11.8 1.1 copy.20
  12.8 1.8 fusion.10
  14.7 2.7 gather_fusion
  17.4 1.9 select_bitcast_fusion
  19.3 1.5 copy.22
  20.8 12.0 %all-to-all-start = ((s32[128,512,8]{0,2,1:T(8,128)}), s32[128,512,8]{0,2,1:T(8,128)S(1)}, u32[]{:S(2)}, u32[]{:S(2)}) async-start(s32[128,512,8]{0,2,1:T(8,128)} %bitcast.75), calls=%async_computation | async-start | bytes 4194304 | tf_op jit(solution)/shard_map/all_to_all | solution.py:55
  32.8 55.4 %gather_fusion.1 = bf16[512,128,128]{2,0,1:T(8,128)(2,1)} fusion(bf16[128,512,128]{2,1,0:T(8,128)(2,1)} %param.8, s32[1024]{0:T(1024)S(1)} %pad_clamp_fusion), kind=kCustom, calls=%fused_computation.1 | custom fusion | bytes 33556480 | tf_op jit(solution)/shard_map/jit(_take)/gather | solution.py:39
  88.2 20.5 %copy_select_fusion = bf16[128,32,4,4,128]{4,0,3,1,2:T(8,128)(2,1)} fusion(bf16[128,32,4,4,128]{4,3,2,1,0:T(4,128)(2,1)} %bitcast.70, pred[32,4,4]{2,0,1:T(8,128)(4,1)S(1)} %copy.24), kind=kLoop, calls=%fused_computation.25 | loop fusion | flops 8388608 | bytes 33554944 | tf_op jit(solution)/shard_map/jit(_take)/select_n | solution.py:39
  108.7 0.0 all-to-all-done
  108.7 0.0 copy-start
  108.7 1.3 copy-done
  110.1 10.2 %all-to-all-start.1 = ((bf16[128,512,128]{2,0,1:T(8,128)(2,1)}), bf16[128,512,128]{2,0,1:T(8,128)(2,1)}, u32[]{:S(2)}, u32[]{:S(2)}) async-start(bf16[128,512,128]{2,0,1:T(8,128)(2,1)} %bitcast.71), calls=%async_computation.1 | async-start | bytes 33554432 | tf_op jit(solution)/shard_map/all_to_all | solution.py:54
  120.3 0.0 all-gather.3.cloned.1.call-start
  120.4 1.7 copy.30
  122.1 225.8 %all-to-all-done.1 = bf16[128,512,128]{2,0,1:T(8,128)(2,1)} async-done(((bf16[128,512,128]{2,0,1:T(8,128)(2,1)}), bf16[128,512,128]{2,0,1:T(8,128)(2,1)}, u32[]{:S(2)}, u32[]{:S(2)}) %all-to-all-start.1) | async-done | bytes 16777248 | tf_op jit(solution)/shard_map/all_to_all | solution.py:54
  347.9 14.1 %copy.26 = bf16[128,128,4,128]{3,1,0,2:T(8,128)(2,1)} copy(bf16[128,128,4,128]{3,1,2,0:T(8,128)(2,1)} %bitcast.22) | data formatting | bytes 33554432 | tf_op jit(solution)/shard_map/all_to_all | solution.py:54
  362.0 168.8 %while.10 = (s32[]{:T(128)}, f32[4,512,128]{2,1,0:T(8,128)S(1)}, s32[4,8,16384]{2,1,0:T(8,128)S(1)}, bf16[4,16384,128]{2,1,0:T(8,128)(2,1)}, s32[]{:T(128)}, /*i...) while((s32[]{:T(128)}, f32[4,512,128]{2,1,0:T(8,128)S(1)}, ...), condition=%wide.region_1.2_spmd, body=%wide.region_0.1_spmd.sunk | while | flops 2348810240 | bytes 6030577 | solution.py:22
  385.4 0.4 constant_dynamic-slice_fusion.9
  385.8 35.5 %fusion.16 = f32[4,512,128]{2,1,0:T(8,128)S(1)} fusion(f32[4,512,128]{2,1,0:T(8,128)S(1)} %get-tuple-element.98, s32[]{:T(128)} %get-tuple-element.97, bf16[4,16384,128]{2,1,0:T(8,128)(2,1)} %get-tuple-element.113, s32[16384]{0:T(1024)S(1)} %bitcast.83, s32[16384]{0:T(1024)S(1)} %bitcast.77, s32[16384]{0:T(1024)S(1)} %bitcast.78, ...), kind=kOutput, calls=%fused_computation.15.clone.1 | convolution fusion | flops 2348810240 | bytes 4981760 | tf_op jit(solution)/shard_map/while/body/eval_jaxpr/dot_general | solution.py:20
  421.3 0.4 constant_dynamic-slice_fusion.9
  421.7 35.5 %fusion.16 = f32[4,512,128]{2,1,0:T(8,128)S(1)} fusion(f32[4,512,128]{2,1,0:T(8,128)S(1)} %get-tuple-element.98, s32[]{:T(128)} %get-tuple-element.97, bf16[4,16384,128]{2,1,0:T(8,128)(2,1)} %get-tuple-element.113, s32[16384]{0:T(1024)S(1)} %bitcast.83, s32[16384]{0:T(1024)S(1)} %bitcast.77, s32[16384]{0:T(1024)S(1)} %bitcast.78, ...), kind=kOutput, calls=%fused_computation.15.clone.1 | convolution fusion | flops 2348810240 | bytes 4981760 | tf_op jit(solution)/shard_map/while/body/eval_jaxpr/dot_general | solution.py:20
  457.3 0.4 constant_dynamic-slice_fusion.9
  457.7 35.5 %fusion.16 = f32[4,512,128]{2,1,0:T(8,128)S(1)} fusion(f32[4,512,128]{2,1,0:T(8,128)S(1)} %get-tuple-element.98, s32[]{:T(128)} %get-tuple-element.97, bf16[4,16384,128]{2,1,0:T(8,128)(2,1)} %get-tuple-element.113, s32[16384]{0:T(1024)S(1)} %bitcast.83, s32[16384]{0:T(1024)S(1)} %bitcast.77, s32[16384]{0:T(1024)S(1)} %bitcast.78, ...), kind=kOutput, calls=%fused_computation.15.clone.1 | convolution fusion | flops 2348810240 | bytes 4981760 | tf_op jit(solution)/shard_map/while/body/eval_jaxpr/dot_general | solution.py:20
  493.2 0.4 constant_dynamic-slice_fusion.9
  493.6 35.5 %fusion.16 = f32[4,512,128]{2,1,0:T(8,128)S(1)} fusion(f32[4,512,128]{2,1,0:T(8,128)S(1)} %get-tuple-element.98, s32[]{:T(128)} %get-tuple-element.97, bf16[4,16384,128]{2,1,0:T(8,128)(2,1)} %get-tuple-element.113, s32[16384]{0:T(1024)S(1)} %bitcast.83, s32[16384]{0:T(1024)S(1)} %bitcast.77, s32[16384]{0:T(1024)S(1)} %bitcast.78, ...), kind=kOutput, calls=%fused_computation.15.clone.1 | convolution fusion | flops 2348810240 | bytes 4981760 | tf_op jit(solution)/shard_map/while/body/eval_jaxpr/dot_general | solution.py:20
  530.9 0.3 multiply_reduce_fusion
  531.2 0.7 fusion.12
  532.0 2.2 fusion.11
  534.2 0.0 all-gather.3.cloned.1.call-update
  534.2 9.0 %all-gather = f32[4,4,512]{2,1,0:T(4,128)S(1)} all-gather(f32[1,4,512]{2,1,0:T(4,128)S(1)} %get-tuple-element.41), channel_id=1, replica_groups=mesh['group'=4,'shard'=32] {'group'}, dimensions={0}, use_global_device_ids=true | all-gather | bytes 40960 | tf_op jit(solution)/shard_map/all_gather | solution.py:63
  543.2 0.6 reshape.61
  543.8 28.0 %all-gather.3.cloned.1.call-done = bf16[16,512,128]{2,1,0:T(8,128)(2,1)} async-done(((bf16[4,512,128]{2,1,0:T(8,128)(2,1)}), bf16[16,512,128]{2,1,0:T(8,128)(2,1)}) %all-gather.3.cloned.1.call-update) | async-done | bytes 2097168 | tf_op jit(solution)/shard_map/all_gather | solution.py:62
  571.9 3.1 copy.39
  (3 shorter events, 0.0 us)
Async XLA Ops:
  20.8 87.9 %all-to-all-start = ((s32[128,512,8]{0,2,1:T(8,128)}), s32[128,512,8]{0,2,1:T(8,128)S(1)}, u32[]{:S(2)}, u32[]{:S(2)}) async-start(s32[128,512,8]{0,2,1:T(8,128)} %bitcast.75), calls=%async_computation | async-start | bytes 4194304 | tf_op jit(solution)/shard_map/all_to_all | solution.py:55
  108.7 1.3 copy-start
  110.1 237.9 %all-to-all-start.1 = ((bf16[128,512,128]{2,0,1:T(8,128)(2,1)}), bf16[128,512,128]{2,0,1:T(8,128)(2,1)}, u32[]{:S(2)}, u32[]{:S(2)}) async-start(bf16[128,512,128]{2,0,1:T(8,128)(2,1)} %bitcast.71), calls=%async_computation.1 | async-start | bytes 33554432 | tf_op jit(solution)/shard_map/all_to_all | solution.py:54
  120.3 451.6 %all-gather.3.cloned.1.call-start = ((), (), s32[]{:S(2)}) async-start(), calls=%async_computation.2 | async-start | bytes 2621440 | tf_op jit(solution)/shard_map/all_gather | solution.py:62
Sparse Core Ops, SparseCore 0:
  534.3 37.5 all-gather.2
where the time goes:
time: 586 us; the launch traced here: 582 us
  waiting for transfers between devices  254 us (43%)
  matrix products  142 us (24%)
  local copies, waits for them, and re-layouts  86.3 us (15%)
  other arithmetic  28.9 us (5%)
  loops' own time  25.2 us (4%)
  starting transfers between devices  22.2 us (4%)
  between operations  14.3 us (2%)
  blocking collectives  9.04 us (2%)
    all_to_all x1, waiting for transfers between devices, body(): lax.all_to_all(pooled, ('group', 'shard'), split_axis=1, concat_axis=0, t...  226 us
    dot_general x4, matrix products, one_table(): jnp.dot(counts.astype(jnp.bfloat16), values, preferred_element_type=jnp.f...  142 us
    gather x1, local copies, waits for them, and re-layouts, body(): pooled = jnp.take(grad_pooled, table_order, axis=1)  55.4 us
    all_gather x1, waiting for transfers between devices, body(): lax.all_gather(part_weights.astype(jnp.float32), 'group', axis=0, tiled=T...  28 us
    another operation x1, loops' own time, expand_rows(): return lax.map(one_table, (tables_first, picks_first))  25.2 us
    select_n x2, other arithmetic, body(): pooled = jnp.take(grad_pooled, table_order, axis=1)  21.2 us
    all_to_all x1, local copies, waits for them, and re-layouts, body(): lax.all_to_all(pooled, ('group', 'shard'), split_axis=1, concat_axis=0, t...  14.1 us
    all_to_all x1, starting transfers between devices, body(): lax.all_to_all(chosen, ('group', 'shard'), split_axis=1, concat_axis=0, t...  12 us
  transfers between devices with their start and end apart: 3, of which 2 were waited for; matrix products, arithmetic and copies ran while one was open for 13% of the time, Pallas kernels for 0%

commit v1 on v0

v1 whole, which is shorter than its diff:
```python
import functools

import jax
import jax.numpy as jnp
from jax import lax
from jax.experimental import pallas as pl
from jax.experimental.pallas import tpu as pltpu
from jax.sharding import PartitionSpec as P

LEARN_RATE = 0.5
EPSILON = 1e-06
LANES = 128
TILE = 16
DIGIT = 64


def pack_kernel(where_ref, turn_ref, grad_ref, rows_ref, lens_ref, out_ref,
                codes, stage, id_stage, stage_sem, id_sem):
    samples, bag, tables = rows_ref.shape
    step = pl.program_id(0)
    steps = pl.num_programs(0)
    slot = lax.rem(step, 2)

    def table_copy(which, t, step_now):
        place = where_ref[step_now * TILE + t]
        dest = lax.div(place, 4)
        q = lax.rem(place, 4)
        return pltpu.make_async_copy(
            stage.at[which, t],
            out_ref.at[dest, pl.ds(pl.multiple_of(q * samples, samples), samples), :],
            stage_sem.at[which, t],
        )

    def id_copy(t):
        place = where_ref[t]
        dest = lax.div(place, 4)
        q = lax.rem(place, 4)
        return pltpu.make_async_copy(
            id_stage.at[t],
            out_ref.at[dest, pl.ds(pl.multiple_of(4 * samples + q * bag, bag), bag), :],
            id_sem,
        )

    @pl.when(step >= 2)
    def _():
        for t in range(TILE):
            table_copy(slot, t, step - 2).wait()

    turn = turn_ref[...]
    for pair in range(samples // (2 * TILE)):
        first = grad_ref[pl.ds(2 * pair * TILE, TILE)].reshape(TILE * TILE, LANES)
        second = grad_ref[pl.ds((2 * pair + 1) * TILE, TILE)].reshape(TILE * TILE, LANES)
        both = jnp.concatenate([first, second], axis=1)
        turned = jnp.dot(turn, both, preferred_element_type=jnp.float32).astype(jnp.bfloat16)
        for half in range(2):
            part = turned[:, half * LANES:(half + 1) * LANES].reshape(TILE, TILE, LANES)
            stage[slot, :, pl.ds((2 * pair + half) * TILE, TILE), :] = part

    for t in range(TILE):
        table_copy(slot, t, step).start()

    @pl.when(step == 0)
    def _():
        for block in range(tables // LANES):
            span = pl.ds(block * LANES, LANES)
            lens = lens_ref[:, span]
            for j in range(bag):
                ids = rows_ref[:, j, span]
                code = jnp.left_shift(DIGIT + (ids & (DIGIT - 1)), ids >> 6)
                code = jnp.where(lens > j, code, 0).astype(jnp.float32)
                codes[pl.ds(block * LANES * bag + j, LANES, stride=bag), :] = code.T
        id_stage[...] = codes[...].reshape(tables, bag, LANES).astype(jnp.bfloat16)

        def send(t, carry):
            id_copy(t).start()
            return carry
        lax.fori_loop(0, tables, send, 0)

    @pl.when(step == steps - 1)
    def _():
        for t in range(TILE):
            table_copy(1 - slot, t, step - 1).wait()
        for t in range(TILE):
            table_copy(slot, t, step).wait()

        def settle(t, carry):
            id_copy(t).wait()
            return carry
        lax.fori_loop(0, tables, settle, 0)


def pack_tables(grad, rows, lens, places):
    samples, tables, width = grad.shape
    bag = rows.shape[1]
    devices = tables // 4
    index = jnp.arange(TILE * TILE, dtype=jnp.int32)
    source = (index % TILE) * TILE + index // TILE
    turn = (source[:, None] == index[None, :]).astype(jnp.bfloat16)
    return pl.pallas_call(
        pack_kernel,
        out_shape=jax.ShapeDtypeStruct((devices, 4 * (samples + bag), width), jnp.bfloat16),
        grid_spec=pltpu.PrefetchScalarGridSpec(
            num_scalar_prefetch=1,
            grid=(tables // TILE,),
            in_specs=[
                pl.BlockSpec((TILE * TILE, TILE * TILE), lambda i, w: (0, 0)),
                pl.BlockSpec((samples, TILE, width), lambda i, w: (0, i, 0)),
                pl.BlockSpec((samples, bag, tables), lambda i, w: (0, 0, 0)),
                pl.BlockSpec((samples, tables), lambda i, w: (0, 0)),
            ],
            out_specs=pl.BlockSpec(memory_space=pl.ANY),
            scratch_shapes=[
                pltpu.VMEM((tables * bag, LANES), jnp.float32),
                pltpu.VMEM((2, TILE, samples, width), jnp.bfloat16),
                pltpu.VMEM((tables, bag, LANES), jnp.bfloat16),
                pltpu.SemaphoreType.DMA((2, TILE)),
                pltpu.SemaphoreType.DMA,
            ],
        ),
        compiler_params=pltpu.CompilerParams(dimension_semantics=("arbitrary",)),
        name="pack_tables",
    )(places, turn, grad, rows, lens)


def decode(code):
    level = jnp.ones(code.shape, jnp.int32)
    big = code >= 1024.0
    code = jnp.where(big, code * 0.0625, code)
    level = jnp.where(big, jnp.left_shift(level, 16), level)
    big = code >= 256.0
    code = jnp.where(big, code * 0.25, code)
    level = jnp.where(big, jnp.left_shift(level, 8), level)
    big = code >= 128.0
    code = jnp.where(big, code * 0.5, code)
    level = jnp.where(big, jnp.left_shift(level, 4), level)
    return code.astype(jnp.int32) - DIGIT, level


def count_rows(low_ref, level_ref, counts, group, column, bag):
    sublane = lax.broadcasted_iota(jnp.int32, (DIGIT, LANES), 0)
    word = jnp.zeros((DIGIT, LANES), jnp.int32)
    for j in range(bag):
        row = group * bag + j
        low = low_ref[pl.ds(row, DIGIT, stride=0), :]
        level = level_ref[pl.ds(row, DIGIT, stride=0), :]
        word = word + jnp.where(low == sublane, level, 0)
    for digit in range(8):
        count = (lax.shift_right_logical(word, 4 * digit) & 15).astype(jnp.float32)
        counts[digit * DIGIT:(digit + 1) * DIGIT, column * LANES:(column + 1) * LANES] = (
            count.astype(jnp.bfloat16)
        )


def update_kernel(start_ref, grad_ref, code_ref, weight_ref, accum_ref, out_w, out_a,
                  total, low_ref, level_ref, counts_a, counts_b):
    block = pl.program_id(1)
    sources, bag = code_ref.shape[0], code_ref.shape[1]
    row_count = total.shape[0]

    @pl.when(block == 0)
    def _():
        total[...] = jnp.zeros_like(total)

    low, level = decode(code_ref[...].astype(jnp.float32))
    low_ref[...] = low.reshape(sources * bag, LANES)
    level_ref[...] = level.reshape(sources * bag, LANES)

    per = counts_a.shape[1] // LANES
    held = (counts_a, counts_b)
    chunks = sources // per
    for chunk in range(chunks + 1):
        if chunk < chunks:
            for column in range(per):
                count_rows(low_ref, level_ref, held[chunk % 2], chunk * per + column, column, bag)
        if chunk > 0:
            values = grad_ref[(chunk - 1) * per:chunk * per].reshape(per * LANES, LANES)
            total[...] += jnp.dot(
                held[(chunk - 1) % 2][...], values, preferred_element_type=jnp.float32
            )

    @pl.when(block == pl.num_programs(1) - 1)
    def _():
        row_grad = total[...]
        mean = jnp.sum(row_grad * row_grad, axis=1, keepdims=True) * (1.0 / LANES)
        old = jnp.broadcast_to(accum_ref[0], (LANES, row_count)).T
        new = old + mean
        step_size = LEARN_RATE / (jnp.sqrt(new) + EPSILON)
        out_w[0] = (weight_ref[0].astype(jnp.float32) - step_size * row_grad).astype(out_w.dtype)
        out_a[0] = new.T[0:1, :]


def update_tables(received, weights, accum, start, quarter, samples, bag):
    devices = received.shape[0]
    row_count, width = weights.shape[1], weights.shape[2]
    sources = 16
    per = 4
    first_code = (4 * samples) // bag
    return pl.pallas_call(
        update_kernel,
        out_shape=(
            jax.ShapeDtypeStruct((quarter, row_count, width), jnp.bfloat16),
            jax.ShapeDtypeStruct((quarter, 1, row_count), jnp.float32),
        ),
        grid_spec=pltpu.PrefetchScalarGridSpec(
            num_scalar_prefetch=1,
            grid=(quarter, devices // sources),
            in_specs=[
                pl.BlockSpec((sources, samples, width), lambda q, k, s: (k, q, 0)),
                pl.BlockSpec((sources, bag, width), lambda q, k, s: (k, first_code + q, 0)),
                pl.BlockSpec((1, row_count, width), lambda q, k, s: (s[0] + q, 0, 0)),
                pl.BlockSpec((1, 1, row_count), lambda q, k, s: (s[0] + q, 0, 0)),
            ],
            out_specs=(
                pl.BlockSpec((1, row_count, width), lambda q, k, s: (q, 0, 0)),
                pl.BlockSpec((1, 1, row_count), lambda q, k, s: (q, 0, 0)),
            ),
            scratch_shapes=[
                pltpu.VMEM((row_count, width), jnp.float32),
                pltpu.VMEM((sources * bag, LANES), jnp.int32),
                pltpu.VMEM((sources * bag, LANES), jnp.int32),
                pltpu.VMEM((row_count, per * LANES), jnp.bfloat16),
                pltpu.VMEM((row_count, per * LANES), jnp.bfloat16),
            ],
        ),
        compiler_params=pltpu.CompilerParams(dimension_semantics=("arbitrary", "arbitrary")),
        name="update_tables",
    )(start, received, received, weights, accum[:, None, :])


def table_places(table_order, groups, shards, quarter):
    tables = table_order.shape[0]
    source = table_order.reshape(shards, groups, quarter).transpose(1, 0, 2).reshape(tables)
    index = jnp.arange(tables, dtype=jnp.int32)
    return jnp.sum(jnp.where(source[None, :] == index[:, None], index[None, :], 0), axis=1)


def body(grad_pooled, bag_rows, bag_lengths, table_order, weights, accum):
    bag = bag_rows.shape[2]
    samples = grad_pooled.shape[0]
    groups = lax.axis_size("group")
    shards = lax.axis_size("shard")
    quarter = weights.shape[0] // groups
    places = table_places(table_order, groups, shards, quarter)
    packed = pack_tables(grad_pooled, jnp.transpose(bag_rows, (0, 2, 1)), bag_lengths, places)
    received = lax.all_to_all(packed, ("group", "shard"), split_axis=0, concat_axis=0, tiled=True)
    start = (lax.axis_index("group") * quarter).astype(jnp.int32).reshape(1)
    part_weights, part_accum = update_tables(
        received, weights, accum, start, quarter, samples, bag
    )
    full_weights = lax.all_gather(part_weights, "group", axis=0, tiled=True)
    full_accum = lax.all_gather(part_accum[:, 0, :], "group", axis=0, tiled=True)
    return (full_weights, full_accum)


def solution(mesh):
    in_specs = (
        P(("group", "shard"), None, None),
        P(("group", "shard"), None, None),
        P(("group", "shard"), None),
        P(),
        P("shard", None, None),
        P("shard", None),
    )
    out_specs = (P("shard", None, None), P("shard", None))
    return jax.shard_map(body, mesh=mesh, in_specs=in_specs, out_specs=out_specs, check_vma=False)
```

time: 586 us -> 416 us (0.71)
  matrix products: 142 us -> 0 us
  Pallas kernels: 0 us -> 94.2 us
  local copies, waits for them, and re-layouts: 86.3 us -> 5.3 us
  other arithmetic: 28.9 us -> 1.53 us
  loops' own time: 25.2 us -> 0 us
  waiting for transfers between devices: 254 us -> 279 us
  starting transfers between devices: 22.2 us -> 11.9 us
    dot_general x4 -> x0, matrix products: 142 us -> none  [one_table(): jnp.dot(counts.astype(jnp.bfloat16), values, preferred_element_type=jnp.f...]
    pallas_call x0 -> x2, Pallas kernels: none -> 94.2 us  [the longest x1 54.5 us: update_tables(): pl.pallas_call(update_kernel, out_shape=(jax.ShapeDtypeStruct((quarter, r...]
    gather x2 -> x0, local copies, waits for them, and re-layouts: 58.1 us -> none  [the longest x1 55.4 us: body(): pooled = jnp.take(grad_pooled, table_order, axis=1)]
    another operation x1 -> x0, loops' own time: 25.2 us -> none  [expand_rows(): return lax.map(one_table, (tables_first, picks_first))]
    select_n x3 -> x0, other arithmetic: 23 us -> none  [the longest x2 21.2 us: body(): pooled = jnp.take(grad_pooled, table_order, axis=1)]
    all_to_all x2 -> x1, waiting for transfers between devices: 226 us -> 249 us  [body(): lax.all_to_all(packed, ('group', 'shard'), split_axis=0, concat_axis=0, t...]
    all_to_all x2 -> x0, local copies, waits for them, and re-layouts: 15.8 us -> none  [the longest x1 14.1 us: body(): lax.all_to_all(pooled, ('group', 'shard'), split_axis=1, concat_axis=0, t...]
    all_to_all x2 -> x1, starting transfers between devices: 22.2 us -> 11.9 us  [body(): lax.all_to_all(packed, ('group', 'shard'), split_axis=0, concat_axis=0, t...]
  transfers between devices with their start and end apart: 3 -> 2, of which waited for: 2 -> 2; matrix products, arithmetic and copies ran while one was open for 13% -> 0% of each run, Pallas kernels for 0% -> 0%
where the time goes in v1:
time: 416 us; the launch traced here: 415 us
  waiting for transfers between devices  279 us (67%)
  Pallas kernels  94.2 us (23%)
  between operations  14.1 us (3%)
  starting transfers between devices  11.9 us (3%)
  blocking collectives  9.25 us (2%)
  local copies, waits for them, and re-layouts  5.3 us (1%)
    all_to_all x1, waiting for transfers between devices, body(): lax.all_to_all(packed, ('group', 'shard'), split_axis=0, concat_axis=0, t...  249 us
    pallas_call x1, Pallas kernels, update_tables(): pl.pallas_call(update_kernel, out_shape=(jax.ShapeDtypeStruct((quarter, r...  54.5 us
    pallas_call x1, Pallas kernels, pack_tables(): pl.pallas_call(pack_kernel, out_shape=jax.ShapeDtypeStruct((devices, 4 *...  39.7 us
    all_gather x1, waiting for transfers between devices, body(): full_weights = lax.all_gather(part_weights, 'group', axis=0, tiled=True)  30 us
    all_to_all x1, starting transfers between devices, body(): lax.all_to_all(packed, ('group', 'shard'), split_axis=0, concat_axis=0, t...  11.9 us
    all_gather x1, blocking collectives, body(): lax.all_gather(part_accum[:, 0, :], 'group', axis=0, tiled=True)  9.25 us
  transfers between devices with their start and end apart: 2, of which 2 were waited for; matrix products, arithmetic and copies ran while one was open for 0% of the time, Pallas kernels for 0%

profile of v1, /device:TPU:1, one launch (start us, length us, event | category | flops | bytes accessed | tf_op | source)
XLA Modules:
  0.0 414.9 jit_solution(10475454298104872272)
XLA Ops:
  7.2 0.8 reshape.34
  8.0 0.1 eq.30
  8.1 0.8 select_reduce_fusion.where_ref
  8.9 0.8 fusion.turn_ref
  9.6 39.7 %pack_tables.1 = bf16[128,544,128]{2,1,0:T(8,128)(2,1)} custom-call(s32[512]{0:T(512)} %select_reduce_fusion.where_ref, bf16[256,256]{1,0:T(8,128)(2,1)} %fusion.turn_ref, bf16[128,512,128]{2,1,0:T(8,128)(2,1)} %grad_ref.1, s32[128,8,512]{2,1,0:T(8,128)} %bitcast.6, s32[128,512]{1,0:T(8,128)} %lens_ref.1), custom_call_target="tpu_custom_call" | custom-call | tf_op jit(solution)/shard_map/pack_tables/pallas_call | solution.py:99
  49.4 0.0 copy-start
  49.4 11.9 %all-to-all-start = ((bf16[128,544,128]{2,1,0:T(8,128)(2,1)}), bf16[128,544,128]{2,1,0:T(8,128)(2,1)}, u32[]{:S(2)}, u32[]{:S(2)}) async-start(bf16[128,544,128]{2,1,0:T(8,128)(2,1)} %pack_tables.1), calls=%async_computation | async-start | bytes 35651584 | tf_op jit(solution)/shard_map/all_to_all | solution.py:245
  61.3 0.0 all-gather.3.cloned.1.call-start
  61.4 0.0 copy-done
  61.4 0.6 broadcast_in_dim.21.accum_ref
  62.0 248.5 %all-to-all-done.grad_ref.code_ref = bf16[128,544,128]{2,1,0:T(8,128)(2,1)} async-done(((bf16[128,544,128]{2,1,0:T(8,128)(2,1)}), bf16[128,544,128]{2,1,0:T(8,128)(2,1)}, u32[]{:S(2)}, u32[]{:S(2)}) %all-to-all-start) | async-done | bytes 17825824 | tf_op jit(solution)/shard_map/all_to_all | solution.py:245
  310.5 54.5 %update_tables.1 = (bf16[4,512,128]{2,1,0:T(8,128)(2,1)}, f32[4,1,512]{2,1,0:T(1,128)}) custom-call(s32[1]{0:T(128)} %bitcast.start_ref, bf16[128,544,128]{2,1,0:T(8,128)(2,1)} %all-to-all-done.grad_ref.code_ref, bf16[128,544,128]{2,1,0:T(8,128)(2,1)} %all-to-all-done.grad_ref.code_ref, bf16[16,512,128]{2,1,0:T(8,128)(2,1)} %weight_ref.1, ...), custom_call_target="tpu_custom_call" | custom-call | tf_op jit(solution)/shard_map/update_tables/pallas_call | solution.py:198
  365.0 0.0 all-gather.3.cloned.1.call-update
  365.0 9.2 %all-gather = f32[16,1,512]{2,1,0:T(1,128)S(1)} all-gather(f32[4,1,512]{2,1,0:T(1,128)} %get-tuple-element.5), channel_id=2, replica_groups=mesh['group'=4,'shard'=32] {'group'}, dimensions={0}, use_global_device_ids=true | all-gather | bytes 40960 | tf_op jit(solution)/shard_map/all_gather | solution.py:251
  374.3 0.6 copy.13
  374.9 30.0 %all-gather.3.cloned.1.call-done = bf16[16,512,128]{2,1,0:T(8,128)(2,1)} async-done(((bf16[4,512,128]{2,1,0:T(8,128)(2,1)}), bf16[16,512,128]{2,1,0:T(8,128)(2,1)}) %all-gather.3.cloned.1.call-update) | async-done | bytes 2097168 | tf_op jit(solution)/shard_map/all_gather | solution.py:250
  404.9 3.1 copy.15
  (2 shorter events, 0.0 us)
Async XLA Ops:
  49.4 12.0 %copy-start = (f32[16,512]{1,0:T(8,128)S(1)}, f32[16,512]{1,0:T(8,128)}, u32[]{:S(2)}) copy-start(f32[16,512]{1,0:T(8,128)} %param.11) | copy-start | bytes 98308
  49.4 261.1 %all-to-all-start = ((bf16[128,544,128]{2,1,0:T(8,128)(2,1)}), bf16[128,544,128]{2,1,0:T(8,128)(2,1)}, u32[]{:S(2)}, u32[]{:S(2)}) async-start(bf16[128,544,128]{2,1,0:T(8,128)(2,1)} %pack_tables.1), calls=%async_computation | async-start | bytes 35651584 | tf_op jit(solution)/shard_map/all_to_all | solution.py:245
  61.3 343.6 %all-gather.3.cloned.1.call-start = ((), (), s32[]{:S(2)}) async-start(), calls=%async_computation.1 | async-start | bytes 2621440 | tf_op jit(solution)/shard_map/all_gather | solution.py:250
Sparse Core Ops, SparseCore 0:
  365.1 39.7 all-gather.2
